TPU v7x, 512 devices: a whole 4x8x8 slice. The times are simulated.
512 devices in a mesh: row: 16 (over z, y_lo), head: 32 (over x, y_hi, core).
Axes of the slice: x: 4, y: 8 (y_hi: 4, y_lo: 2; y = y_hi * 2 + y_lo), z: 8, core: 2. Of those that a mesh axis runs over, the one named last changes fastest.
Arguments:
- q_nope: bfloat16 [2048, 16384], P('row', 'head'), may hold values from -6 to 6
- q_rope: bfloat16 [2048, 8192], P('row', 'head'), may hold values from -192 to 192
- latent_keys: bfloat16 [512, 4096], P(None, 'row'), may hold values from -6 to 6
- rope_keys: bfloat16 [64, 4096], P(None, 'row'), may hold values from -8 to 8
- panel_block: int32 [16], replicated, may hold values from 0 to 63, as said below
- query_pos: int32 [2048], P('row'), may hold values from 1 to 16383
- w_uk: bfloat16 [128, 128, 512], P('head'), may hold values from -0.5 to 0.5
- w_uv: bfloat16 [128, 512, 128], P('head'), may hold values from -1 to 1
- w_out: bfloat16 [7168, 16384], P('row', 'head'), may hold values from -0.09375 to 0.09375
Outputs:
- attn_out: bfloat16 [2048, 7168], P(('row', 'head'))
Inputs may be any that keep to these rules, and one draw needn't show every extreme that they name: `panel_block`: distinct block numbers; 0 and the largest allowed block are always among them.
All inputs are finite; a program needn't handle non-finite values.
Results may differ from a plain program's by a relative error of at most 0.025.
Values may be sent and summed in bfloat16 or wider, within the bound.
A program may use at most 64 MiB of HBM per device.

v0:
```python
import jax
import jax.numpy as jnp
from jax import lax
from jax.sharding import Mesh
from jax.sharding import PartitionSpec as P

NOPE = 128
ROPE = 64
LATENT = 512
VHEAD = 128
PANEL = 256
HEAD = ("head_0", "head_1", "head_2")
ROW_HEAD = ("row", "head_0", "head_1", "head_2")


softmax_scale = 192.0 ** (-0.5)
lowest_start = -1e30


def in_one_piece(arrays, axis, dim, along):
    ends, at = ([], 0)
    for a in arrays[:-1]:
        at += a.shape[along]
        ends.append(at)
    both = jnp.concatenate(arrays, axis=along)
    return tuple(jnp.split(lax.all_gather(both, axis, axis=dim, tiled=True), ends, axis=along))


def from_everyone(x, axis):
    count = lax.axis_size(axis)
    return lax.all_to_all(jnp.broadcast_to(x[None], (count, *x.shape)), axis, 0, 0, tiled=True)


def laid_out(pieces, dim):
    pieces = jnp.moveaxis(pieces, 0, dim)
    lengths = pieces.shape
    return pieces.reshape(*lengths[:dim], lengths[dim] * lengths[dim + 1], *lengths[dim + 2 :])


def collect(x, axis, dim):
    pieces = from_everyone(x, axis)
    return laid_out(pieces, dim)


def split_up(x, dim, count):
    before, after = (x.shape[:dim], x.shape[dim + 1 :])
    return jnp.moveaxis(x.reshape(*before, count, -1, *after), dim, 0)


def summed_on_arrival(x, axis, dim):
    pieces = split_up(x, dim, lax.axis_size(axis))
    arrived = lax.all_to_all(pieces, axis, split_axis=0, concat_axis=0, tiled=True)
    return arrived.astype(jnp.float32).sum(axis=0)


def sum_by_axis(x, axes, dim):
    far, near = axes
    pieces = split_up(x, dim, lax.axis_size(far))
    nearer = summed_on_arrival(pieces, near, dim + 1)
    arrived = lax.all_to_all(
        nearer.astype(jnp.bfloat16), far, split_axis=0, concat_axis=0, tiled=True
    )
    return arrived.astype(jnp.float32).sum(axis=0)


def on_device(q_nope, q_rope, latent_keys, rope_keys, panel_block, query_pos, w_uk, w_uv, w_out):
    row_count = q_nope.shape[0]
    head_count = w_uk.shape[0]
    panel_count = panel_block.shape[0]
    nope_heads = q_nope.reshape(row_count, head_count, NOPE)
    query_latent = jnp.einsum(
        "rhn,hnl->hrl", nope_heads, w_uk, preferred_element_type=jnp.float32
    ).astype(jnp.bfloat16)
    query_latent = query_latent.reshape(head_count * row_count, LATENT)
    query_rope = jnp.transpose(q_rope.reshape(row_count, head_count, ROPE), (1, 0, 2)).reshape(
        head_count * row_count, ROPE
    )
    flat_pos = jnp.tile(query_pos, head_count)
    panel_ids = jnp.arange(panel_count, dtype=jnp.int32)
    flat_rows = head_count * row_count
    running_max = jnp.full((flat_rows,), lowest_start, jnp.float32)
    latent_piece, rope_piece = in_one_piece((latent_keys, rope_keys), "row", 1, 0)
    width = latent_piece.shape[1]
    columns = jnp.arange(width, dtype=jnp.int32)
    owner = columns // PANEL
    block_of = jnp.sum(
        jnp.where(owner[:, None] == panel_ids[None, :], panel_block[None, :], 0), axis=1
    )
    key_pos = block_of * PANEL + columns % PANEL
    scores = jnp.dot(query_latent, latent_piece, preferred_element_type=jnp.float32)
    scores = scores + jnp.dot(query_rope, rope_piece, preferred_element_type=jnp.float32)
    visible = key_pos[None, :] <= flat_pos[:, None]
    scores = jnp.where(visible, scores * softmax_scale, -jnp.inf)
    new_max = jnp.maximum(running_max, jnp.max(scores, axis=1))
    weights = jnp.exp(scores - new_max[:, None])
    denominator = jnp.sum(weights, axis=1)
    update = lax.dot_general(
        weights.astype(jnp.bfloat16),
        latent_piece,
        (((1,), (1,)), ((), ())),
        preferred_element_type=jnp.float32,
    )
    accumulated = update
    running_max, denominator, accumulated = (new_max, denominator, accumulated)
    mixed_latent = (
        (accumulated / denominator[:, None])
        .astype(jnp.bfloat16)
        .reshape(head_count, row_count, LATENT)
    )
    values = jnp.einsum(
        "hrl,hlv->rhv", mixed_latent, w_uv, preferred_element_type=jnp.float32
    ).astype(jnp.bfloat16)
    values = values.reshape(row_count, head_count * VHEAD)
    row_devices = lax.axis_size("row")
    head_devices = lax.axis_size(HEAD)
    sub_rows = row_count // head_devices
    feature_slice = w_out.shape[0]
    partial_out = lax.dot_general(
        collect(values, "row", 0),
        w_out,
        (((1,), (1,)), ((), ())),
        preferred_element_type=jnp.float32,
    )
    partial_out = partial_out.reshape(row_devices, head_devices, sub_rows, feature_slice)
    summed = sum_by_axis(partial_out.astype(jnp.bfloat16), (("head_0", "head_1"), "head_2"), 1)
    summed = summed.reshape(row_devices, sub_rows, feature_slice).astype(jnp.bfloat16)
    returned = lax.all_to_all(summed, "row", split_axis=0, concat_axis=2, tiled=True)
    return returned.reshape(sub_rows, row_devices * feature_slice)


def solution(mesh):
    finer = Mesh(
        mesh.devices.reshape(mesh.shape["row"], 4, 4, 2), ("row", "head_0", "head_1", "head_2")
    )
    return jax.shard_map(
        on_device,
        mesh=finer,
        in_specs=(
            P("row", HEAD),
            P("row", HEAD),
            P(None, "row"),
            P(None, "row"),
            P(),
            P("row"),
            P(HEAD, None, None),
            P(HEAD, None, None),
            P("row", HEAD),
        ),
        out_specs=P(ROW_HEAD, None),
        check_vma=False,
    )
```

profile of v0, /device:TPU:8, one launch (start us, length us, event | category | flops | bytes accessed | tf_op | source)
XLA Modules:
  0.0 269.7 jit_solution(8531192472056866777)
XLA Ops:
  6.5 0.0 copy-start
  6.5 0.0 all-gather.2.cloned.1.call-start
  6.5 1.8 pad_maximum_fusion
  8.3 0.0 all-gather.2.cloned.1.call-update
  8.3 1.0 copy.45
  9.3 0.8 select_reduce_fusion
  10.1 0.7 broadcast_bitcast_fusion
  10.7 0.0 copy-done
  10.7 1.2 convolution_convert_fusion
  11.9 114.5 %all-gather.2.cloned.1.call-done = bf16[576,4096]{1,0:T(8,128)(2,1)} async-done(((bf16[576,256]{1,0:T(8,128)(2,1)}), bf16[576,4096]{1,0:T(8,128)(2,1)}) %all-gather.2.cloned.1.call-update) | async-done | bytes 4718608 | tf_op jit(solution)/shard_map/all_gather | solution.py:26
  126.4 4.7 %fusion.8 = f32[512,4096]{1,0:T(8,128)S(1)} fusion(bf16[512,512]{1,0:T(8,128)(2,1)S(1)} %bitcast.58, bf16[576,4096]{1,0:T(8,128)(2,1)} %all-gather.2.cloned.1.call-done), kind=kOutput, calls=%fused_computation.9 | convolution fusion | flops 2147483648 | bytes 13107200 | tf_op jit(solution)/shard_map/dot_general | solution.py:90
  131.1 0.0 copy-done.1
  131.1 2.1 fusion.39
  133.2 1.3 fusion.2
  134.5 2.4 fusion.20
  136.9 0.0 copy-done.2
  136.9 0.3 convolution_convert_fusion.1
  137.3 0.1 copy.49
  137.4 0.2 broadcast_in_dim.37
  137.6 0.0 copy-start.3
  137.6 56.4 %all_to_all.30 = bf16[16,128,512]{2,1,0:T(8,128)(2,1)S(1)} all-to-all(bf16[16,128,512]{2,1,0:T(8,128)(2,1)S(1)} %broadcast_in_dim.37), channel_id=1, replica_groups=mesh['row'=16,'head_0'=4,'head_1'=4,'head_2'=2] {'row'}, dimensions={0} | all-to-all | bytes 4194304 | tf_op jit(solution)/shard_map/all_to_all | solution.py:31
  194.0 1.2 copy.50
  195.2 4.0 %fusion.12 = bf16[16,32,4,448]{3,1,2,0:T(8,128)(2,1)} fusion(bf16[16,32,4,512]{3,0,2,1:T(8,128)(2,1)S(1)} %bitcast.59, bf16[448,512]{1,0:T(8,128)(2,1)S(1)} %copy-done.3), kind=kOutput, calls=%fused_computation.14 | convolution fusion | flops 940441600 | bytes 4390912 | tf_op jit(solution)/shard_map/dot_general | solution.py:118
  199.3 2.8 %reshape.72 = bf16[16,16,2,4,448]{4,2,1,3,0:T(2,128)(2,1)S(1)} reshape(bf16[16,32,4,448]{3,1,2,0:T(8,128)(2,1)} %fusion.12) | data formatting | bytes 3670016 | tf_op jit(solution)/shard_map/reshape | solution.py:47
  202.1 0.5 copy.77
  202.5 5.4 %all_to_all.31 = bf16[2,16,16,1,4,448]{5,1,4,2,3,0:T(8,128)(2,1)S(1)} all-to-all(bf16[2,16,16,1,4,448]{5,1,4,2,3,0:T(8,128)(2,1)S(1)} %bitcast.56), channel_id=1, replica_groups=mesh['row'=16,'head_0'=4,'head_1'=4,'head_2'=2] {'head_2'}, dimensions={0} | all-to-all | bytes 3670016 | tf_op jit(solution)/shard_map/all_to_all | solution.py:52
  208.0 1.8 reduce_sum.46
  209.7 2.0 copy.54
  211.8 37.2 %all_to_all.32 = bf16[16,16,1,4,448]{4,3,1,2,0:T(4,128)(2,1)S(1)} all-to-all(bf16[16,16,1,4,448]{4,3,1,2,0:T(4,128)(2,1)S(1)} %copy.54), channel_id=1, replica_groups=mesh['row'=16,'head_0'=4,'head_1'=4,'head_2'=2] {'head_0','head_1'}, dimensions={0} | all-to-all | bytes 1835008 | tf_op jit(solution)/shard_map/all_to_all | solution.py:60
  249.0 0.5 reduce_sum.48
  249.5 12.6 %all_to_all.33 = bf16[16,4,448]{2,1,0:T(4,128)(2,1)S(1)} all-to-all(bf16[16,4,448]{2,1,0:T(4,128)(2,1)S(1)} %reduce_sum.48), channel_id=1, replica_groups=mesh['row'=16,'head_0'=4,'head_1'=4,'head_2'=2] {'row'}, dimensions={0} | all-to-all | bytes 114688 | tf_op jit(solution)/shard_map/all_to_all | solution.py:127
  262.1 0.8 reshape.74
  (7 shorter events, 0.0 us)
Async XLA Ops:
  6.5 4.2 %copy-start = (bf16[4,128,512]{2,1,0:T(8,128)(2,1)S(1)}, bf16[4,128,512]{2,1,0:T(8,128)(2,1)}, u32[]{:S(2)}) copy-start(bf16[4,128,512]{2,1,0:T(8,128)(2,1)} %param.15) | copy-start | bytes 1572868
  6.5 119.9 %all-gather.2.cloned.1.call-start = ((), (), s32[]{:S(2)}) async-start(), calls=%async_computation.4 | async-start | bytes 5013504 | tf_op jit(solution)/shard_map/all_gather | solution.py:26
  126.4 4.7 %copy-start.1 = (bf16[576,4096]{1,0:T(8,128)(2,1)S(1)}, bf16[576,4096]{1,0:T(8,128)(2,1)}, u32[]{:S(2)}) copy-start(bf16[576,4096]{1,0:T(8,128)(2,1)} %all-gather.2.cloned.1.call-done) | copy-start | bytes 14155780
  134.5 2.4 copy-start.2
  137.6 57.6 %copy-start.3 = (bf16[448,512]{1,0:T(8,128)(2,1)S(1)}, bf16[448,512]{1,0:T(8,128)(2,1)}, u32[]{:S(2)}) copy-start(bf16[448,512]{1,0:T(8,128)(2,1)} %param.17) | copy-start | bytes 1376260
Sparse Core Ops, SparseCore 0:
  9.3 117.0 all-gather.1
where the time goes:
time: 270 us
  waiting for transfers between devices  115 us (43%)
  blocking collectives  112 us (41%)
  matrix products  14.7 us (5%)
  between operations  13.5 us (5%)
  local copies, waits for them, and re-layouts  9.19 us (3%)
  other arithmetic  6.12 us (2%)
    all_gather x1, waiting for transfers between devices, in_one_piece(): lax.all_gather(both, axis, axis=dim, tiled=True)  114 us
    all_to_all x1, blocking collectives, from_everyone(): lax.all_to_all(jnp.broadcast_to(x[None], (count, *x.shape)), axis, 0, 0,...  56.4 us
    all_to_all x1, blocking collectives, sum_by_axis(): lax.all_to_all(nearer.astype(jnp.bfloat16), far, split_axis=0, concat_axi...  37.2 us
    all_to_all x1, blocking collectives, on_device(): lax.all_to_all(summed, 'row', split_axis=0, concat_axis=2, tiled=True)  12.6 us
    all_to_all x1, blocking collectives, summed_on_arrival(): lax.all_to_all(pieces, axis, split_axis=0, concat_axis=0, tiled=True)  5.42 us
  transfers between devices with their start and end apart: 1, of which 1 were waited for; matrix products, arithmetic and copies ran while one was open for 1% of the time, Pallas kernels for 0%

commit v1 on v0

v1 whole, which is shorter than its diff:
```python
import functools

import jax
import jax.numpy as jnp
from jax import lax
from jax.experimental import pallas as pl
from jax.experimental.pallas import tpu as pltpu
from jax.sharding import Mesh
from jax.sharding import PartitionSpec as P

NOPE = 128
ROPE = 64
LATENT = 512
VHEAD = 128
PANEL = 256
AXES = ("z", "ylo", "x", "yhi", "core")
ROW = ("z", "ylo")
HEAD = ("x", "yhi", "core")
MESH = pl.DeviceIdType.MESH
NZ, NX, NY = 8, 4, 4
DZ = (0, 1, 7, 2, 6, 3, 5, 4)
OFF = (0, -1, 1, -2, 2, -3, 3, 4)
LIMIT = ((4, 3), (3, 4))

softmax_scale = 192.0 ** (-0.5)


def mod(a, n):
    return lax.rem(a + n, n)


def remote(src, dst, send_sem, recv_sem, device):
    return pltpu.make_async_remote_copy(
        src_ref=src,
        dst_ref=dst,
        send_sem=send_sem,
        recv_sem=recv_sem,
        device_id=device,
        device_id_type=MESH,
    )


def meet(peers):
    barrier = pltpu.get_barrier_semaphore()
    for peer in peers:
        pl.semaphore_signal(barrier, inc=1, device_id=peer, device_id_type=MESH)
    pl.semaphore_wait(barrier, len(peers))


def gather_kernel(lat, rope, out, kv, send_sem, z_sem, x_sem, y_sem, c_sem, load_sem, out_sem):
    z, ylo, x, yhi, c = (lax.axis_index(a) for a in AXES)
    way = 1 - 2 * c
    here = z * 2 + ylo

    def piece(panel, half, part):
        return (panel * 2 + half) * 4 + part

    loads = []
    for half in range(2):
        lanes = pl.ds(128 * half, 128)
        for part in range(3):
            loads.append((lat.at[pl.ds(144 * part, 144), lanes], kv.at[piece(here, half, part)]))
        last = kv.at[piece(here, half, 3)]
        loads.append((lat.at[pl.ds(432, 80), lanes], last.at[pl.ds(0, 80)]))
        loads.append((rope.at[:, lanes], last.at[pl.ds(80, 64)]))
    loads = [pltpu.make_async_copy(s, d, load_sem.at[i]) for i, (s, d) in enumerate(loads)]
    for load in loads:
        load.start()
    y_up = {"ylo": 1 - ylo, "yhi": mod(yhi + ylo, NY)}
    y_down = {"ylo": 1 - ylo, "yhi": mod(yhi + ylo - 1, NY)}
    peers = [{"z": mod(z + d, NZ)} for d in range(1, NZ)]
    peers += [{"x": mod(x + 1, NX)}, {"x": mod(x - 1, NX)}, y_up, y_down, {"core": 1 - c}]
    meet(peers)
    for load in loads:
        load.wait()

    def copy_out(panel, half, slot):
        copy = pltpu.make_async_copy(
            kv.at[pl.ds(piece(panel, half, 0), 4)],
            out.at[:, :, pl.ds(pl.multiple_of(panel * PANEL + half * 128, 128), 128)],
            out_sem.at[slot],
        )
        copy.start()
        outs.append(copy)

    outs = []
    mine = kv.at[piece(here, c, x)]
    for d in (1, 7, 2, 6, 3, 5, 4):
        remote(mine, mine, send_sem.at[0], z_sem.at[DZ.index(d)], {"z": mod(z + d, NZ)}).start()

    def panel_of(k, low):
        return mod(z - DZ[k], NZ) * 2 + low

    def spread_y(k, part, turn):
        ref = kv.at[piece(panel_of(k, ylo), c, part)]
        to = {"ylo": 1 - ylo, "yhi": mod(yhi + ylo - lax.rem(part, 2), NY)}
        remote(ref, ref, send_sem.at[0], y_sem.at[k, turn], to).start()

    def spread_core(panel, part, slot):
        ref = kv.at[piece(panel, c, part)]
        remote(ref, ref, send_sem.at[0], c_sem.at[slot], {"core": 1 - c}).start()

    def spread_x(k, part, turn, step):
        ref = kv.at[piece(panel_of(k, ylo), c, part)]
        remote(ref, ref, send_sem.at[0], x_sem.at[k, turn], {"x": mod(x + step, NX)}).start()

    def arrived(ref, sem):
        remote(ref, ref, send_sem.at[0], sem, {"core": 1 - c}).wait_recv()

    parts = (x, mod(x - way, NX), mod(x + way, NX), mod(x + 2, NX))

    def stage_z(k):
        if k:
            arrived(kv.at[piece(panel_of(k, ylo), c, x)], z_sem.at[k])
            spread_x(k, x, 0, way)
            spread_x(k, x, 1, -way)
        spread_y(k, x, 0)
        if k:
            spread_core(panel_of(k, ylo), x, k)

    def stage_x(k, turns):
        for turn in turns:
            part = parts[turn + 1]
            if k:
                arrived(kv.at[piece(panel_of(k, ylo), c, part)], x_sem.at[k, turn])
            if k and turn == 0:
                spread_x(k, part, 2, way)
            spread_y(k, part, turn + 1)
            if k:
                spread_core(panel_of(k, ylo), part, k)
        if 2 in turns:
            copy_out(panel_of(k, ylo), c, 2 * k)

    def stage_y(k):
        panel = panel_of(k, 1 - ylo)
        for turn in range(4):
            arrived(kv.at[piece(panel, c, parts[turn])], y_sem.at[k, turn])
            spread_core(panel, parts[turn], 8 + k)
        copy_out(panel, c, 16 + 2 * k)

    def stage_core(k):
        panel = panel_of(k, ylo)
        if k:
            arrived(kv.at[pl.ds(piece(panel, 1 - c, 0), 4)], c_sem.at[k])
        copy_out(panel, 1 - c, 2 * k + 1)
        panel = panel_of(k, 1 - ylo)
        arrived(kv.at[pl.ds(piece(panel, 1 - c, 0), 4)], c_sem.at[8 + k])
        copy_out(panel, 1 - c, 16 + 2 * k + 1)

    for t in range(NZ + 4):
        if t < NZ:
            stage_z(t)
        if 0 <= t - 1 < NZ:
            stage_x(t - 1, (0, 1))
        if 0 <= t - 2 < NZ:
            stage_x(t - 2, (2,))
        if 0 <= t - 3 < NZ:
            stage_y(t - 3)
        if 0 <= t - 4 < NZ:
            stage_core(t - 4)
    for copy in outs:
        copy.wait()
    sent = kv.at[pl.ds(0, 7 + 21 + 32 + 28 + 32)]
    remote(sent, sent, send_sem.at[0], c_sem.at[0], {"core": 1 - c}).wait_send()


def gather_cache(lat, rope):
    return pl.pallas_call(
        gather_kernel,
        out_shape=jax.ShapeDtypeStruct((4, 144, 16 * PANEL), jnp.bfloat16),
        in_specs=[pl.BlockSpec(memory_space=pl.ANY)] * 2,
        out_specs=pl.BlockSpec(memory_space=pl.ANY),
        scratch_shapes=[
            pltpu.VMEM((128, 144, 128), jnp.bfloat16),
            pltpu.SemaphoreType.DMA((1,)),
            pltpu.SemaphoreType.DMA((8,)),
            pltpu.SemaphoreType.DMA((8, 3)),
            pltpu.SemaphoreType.DMA((8, 4)),
            pltpu.SemaphoreType.DMA((16,)),
            pltpu.SemaphoreType.DMA((10,)),
            pltpu.SemaphoreType.DMA((32,)),
        ],
        compiler_params=pltpu.CompilerParams(collective_id=0, has_side_effects=True),
        name="gather_cache",
    )(lat, rope)


def project_kernel(
    vals, w_near, w_far, out,
    vall, acc, cs, cr, xs, xr, xown, tb, ys, yr, yown, fs, fr,
    send_sem, ag_sem, c_sem, x_sem, y_sem, f_sem,
):
    z, ylo, x, yhi, c = (lax.axis_index(a) for a in AXES)
    partner = {"core": 1 - c}
    peers = [{"z": mod(z + d, NZ)} for d in range(1, NZ)]
    peers += [{"x": mod(x + d, NX)} for d in range(1, NX)]
    peers += [{"yhi": mod(yhi + d, NY)} for d in range(1, NY)]
    peers += [partner]
    meet(peers)
    steps = ({"z": mod(z + 1, NZ)}, {"z": mod(z - 1, NZ)})

    for sub in range(2):
        for side in range(2):
            remote(
                vals.at[sub], vall.at[2 * z + sub], send_sem.at[0], ag_sem.at[side, 0, sub], steps[side]
            ).start()

    def arrived(ref, sem):
        remote(ref, ref, send_sem.at[0], sem, partner).wait_recv()

    def land(m):
        dist = abs(OFF[m])
        source = mod(z + OFF[m], NZ)
        for sub in range(2):
            side = sub if dist == 4 else (0 if OFF[m] < 0 else 1)
            ref = vall.at[2 * source + sub]
            arrived(ref, ag_sem.at[side, dist - 1, sub])
            if dist + 1 <= LIMIT[side][sub]:
                remote(ref, ref, send_sem.at[0], ag_sem.at[side, dist, sub], steps[side]).start()
        return source

    def multiply(m):
        if m:
            source = land(m)
            rows = vall[pl.ds(2 * source, 2)].reshape(128, 512)
        else:
            rows = vals[...].reshape(128, 512)
        for j, w in enumerate((w_near, w_far)):
            product = lax.dot_general(
                rows, w[...], (((1,), (1,)), ((), ())), preferred_element_type=jnp.float32
            )
            acc[m, :, j] = product.reshape(2, 64, 448)
            cs[m, j] = acc[m, 1 - c, j].astype(jnp.bfloat16)
        remote(cs.at[m], cr.at[m], send_sem.at[1], c_sem.at[m], partner).start()

    def reduce_core(m):
        arrived(cr.at[m], c_sem.at[m])
        for d in (2, 1, 3, 0):
            at = pl.ds(pl.multiple_of(16 * mod(x + d, NX), 16), 16)
            for j in range(2):
                both = acc[m, c, j, at, :] + cr[m, j, at, :].astype(jnp.float32)
                if d:
                    xs[m, d - 1, j] = both.astype(jnp.bfloat16)
                else:
                    xown[m, j] = both
            if d:
                remote(
                    xs.at[m, d - 1], xr.at[m, d - 1], send_sem.at[2], x_sem.at[m, d - 1],
                    {"x": mod(x + d, NX)},
                ).start()

    def reduce_x(m):
        batch, k = divmod(m, 4)
        for d in range(3):
            arrived(xr.at[m, d], x_sem.at[m, d])
        for j in range(2):
            total = xown[m, j]
            for d in range(3):
                total = total + xr[m, d, j].astype(jnp.float32)
            tb[batch, j, 16 * k : 16 * k + 16, :] = total.astype(jnp.bfloat16)
        if k < 3:
            return
        row = lax.broadcasted_iota(jnp.int32, (16, 64), 0)
        column = lax.broadcasted_iota(jnp.int32, (16, 64), 1)
        first = (row // 4) * 16 + row % 4
        for d in (2, 1, 3, 0):
            to = mod(yhi + d, NY)
            pick = jnp.where(column == first + 4 * to, 1.0, 0.0).astype(jnp.bfloat16)
            for j in range(2):
                chosen = jnp.dot(pick, tb[batch, j], preferred_element_type=jnp.float32)
                if d:
                    ys[batch, d - 1, j] = chosen.astype(jnp.bfloat16)
                else:
                    yown[batch, j] = chosen
            if d:
                remote(
                    ys.at[batch, d - 1], yr.at[batch, d - 1], send_sem.at[3],
                    y_sem.at[batch, d - 1], {"yhi": to},
                ).start()

    def reduce_y(batch):
        for d in range(3):
            arrived(yr.at[batch, d], y_sem.at[batch, d])
        for j in range(2):
            total = yown[batch, j]
            for d in range(3):
                total = total + yr[batch, d, j].astype(jnp.float32)
            for k in range(4):
                rows = total[4 * k : 4 * k + 4].astype(jnp.bfloat16)
                if batch or k:
                    fs[4 * batch + k, j] = rows
                else:
                    fr[z, j] = rows
        for k in range(4):
            m = 4 * batch + k
            if m:
                remote(
                    fs.at[m], fr.at[z], send_sem.at[4], f_sem.at[m], {"z": mod(z + OFF[m], NZ)}
                ).start()

    for t in range(NZ + 2):
        if t < NZ:
            multiply(t)
        if 0 <= t - 1 < NZ:
            reduce_core(t - 1)
        if 0 <= t - 2 < NZ:
            reduce_x(t - 2)
        if t == 7:
            reduce_y(0)
    reduce_y(1)
    for m in range(1, NZ):
        arrived(fr.at[mod(z - OFF[m], NZ)], f_sem.at[m])
    for j in range(2):
        out[:, lax.rem(ylo + j, 2)] = fr[:, j]
    for ref, i in ((vall.at[pl.ds(0, 14)], 0), (cs, 1), (xs, 2), (ys, 3), (fs.at[pl.ds(1, 7)], 4)):
        remote(ref, ref, send_sem.at[i], c_sem.at[0], partner).wait_send()


def project(vals, w_near, w_far):
    bf, f32 = jnp.bfloat16, jnp.float32
    return pl.pallas_call(
        project_kernel,
        out_shape=jax.ShapeDtypeStruct((8, 2, 4, 448), bf),
        in_specs=[pl.BlockSpec(memory_space=pltpu.VMEM)] * 3,
        out_specs=pl.BlockSpec(memory_space=pltpu.VMEM),
        scratch_shapes=[
            pltpu.VMEM((16, 64, 512), bf),
            pltpu.VMEM((8, 2, 2, 64, 448), f32),
            pltpu.VMEM((8, 2, 64, 448), bf),
            pltpu.VMEM((8, 2, 64, 448), bf),
            pltpu.VMEM((8, 3, 2, 16, 448), bf),
            pltpu.VMEM((8, 3, 2, 16, 448), bf),
            pltpu.VMEM((8, 2, 16, 448), f32),
            pltpu.VMEM((2, 2, 64, 448), bf),
            pltpu.VMEM((2, 3, 2, 16, 448), bf),
            pltpu.VMEM((2, 3, 2, 16, 448), bf),
            pltpu.VMEM((2, 2, 16, 448), f32),
            pltpu.VMEM((8, 2, 4, 448), bf),
            pltpu.VMEM((8, 2, 4, 448), bf),
            pltpu.SemaphoreType.DMA((5,)),
            pltpu.SemaphoreType.DMA((2, 4, 2)),
            pltpu.SemaphoreType.DMA((8,)),
            pltpu.SemaphoreType.DMA((8, 3)),
            pltpu.SemaphoreType.DMA((2, 3)),
            pltpu.SemaphoreType.DMA((8,)),
        ],
        compiler_params=pltpu.CompilerParams(
            collective_id=1, has_side_effects=True, vmem_limit_bytes=48 << 20
        ),
        name="project",
    )(vals, w_near, w_far)


def on_device(q_nope, q_rope, latent_keys, rope_keys, panel_block, query_pos, w_uk, w_uv, w_out):
    row_count = q_nope.shape[0]
    head_count = w_uk.shape[0]
    nope_heads = q_nope.reshape(row_count, head_count, NOPE)
    query_latent = jnp.einsum(
        "rhn,hnl->hrl", nope_heads, w_uk, preferred_element_type=jnp.float32
    ).astype(jnp.bfloat16)
    query_latent = query_latent.reshape(head_count * row_count, LATENT)
    query_rope = jnp.transpose(q_rope.reshape(row_count, head_count, ROPE), (1, 0, 2)).reshape(
        head_count * row_count, ROPE
    )
    flat_pos = jnp.tile(query_pos, head_count)
    panel_count = panel_block.shape[0]
    panel_ids = jnp.arange(panel_count, dtype=jnp.int32)
    columns = jnp.arange(panel_count * PANEL, dtype=jnp.int32)
    owner = columns // PANEL
    block_of = jnp.sum(
        jnp.where(owner[:, None] == panel_ids[None, :], panel_block[None, :], 0), axis=1
    )
    key_pos = block_of * PANEL + columns % PANEL

    both = gather_cache(latent_keys, rope_keys).reshape(LATENT + ROPE, panel_count * PANEL)
    w_far = lax.ppermute(w_out, "ylo", [(0, 1), (1, 0)])
    latent_all, rope_all = both[:LATENT], both[LATENT:]
    scores = jnp.dot(query_latent, latent_all, preferred_element_type=jnp.float32)
    scores = scores + jnp.dot(query_rope, rope_all, preferred_element_type=jnp.float32)
    visible = key_pos[None, :] <= flat_pos[:, None]
    scores = jnp.where(visible, scores * softmax_scale, -jnp.inf)
    top = jnp.max(scores, axis=1)
    weights = jnp.exp(scores - top[:, None])
    denominator = jnp.sum(weights, axis=1)
    mixed = lax.dot_general(
        weights.astype(jnp.bfloat16),
        latent_all,
        (((1,), (1,)), ((), ())),
        preferred_element_type=jnp.float32,
    )
    mixed_latent = (
        (mixed / denominator[:, None])
        .astype(jnp.bfloat16)
        .reshape(head_count, row_count, LATENT)
    )
    values = jnp.einsum(
        "hrl,hlv->rhv", mixed_latent, w_uv, preferred_element_type=jnp.float32
    ).astype(jnp.bfloat16)
    values = values.reshape(NX, NY, 2, 4, head_count * VHEAD)
    values = jnp.transpose(values, (2, 0, 1, 3, 4)).reshape(2, 64, head_count * VHEAD)
    pieces = project(values, w_out, w_far)
    return jnp.transpose(pieces, (2, 0, 1, 3)).reshape(4, 7168)


def solution(mesh):
    finer = Mesh(mesh.devices.reshape(NZ, 2, NX, NY, 2), AXES)
    return jax.shard_map(
        on_device,
        mesh=finer,
        in_specs=(
            P(ROW, HEAD),
            P(ROW, HEAD),
            P(None, ROW),
            P(None, ROW),
            P(),
            P(ROW),
            P(HEAD, None, None),
            P(HEAD, None, None),
            P(ROW, HEAD),
        ),
        out_specs=P(ROW + HEAD, None),
        check_vma=False,
    )
```

time: 270 us -> 104 us (0.39)
  the two profiles are of different devices: /device:TPU:8 before, /device:TPU:64 now
where the time goes in v1:
time: 104 us; the launch traced here: 103 us
  Pallas kernels  84.2 us (81%)
  matrix products  10.7 us (10%)
  starting transfers between devices  3.61 us (3%)
  local copies, waits for them, and re-layouts  2.69 us (3%)
  other arithmetic  2.08 us (2%)
    pallas_call x1, Pallas kernels, project(): pl.pallas_call(project_kernel, out_shape=jax.ShapeDtypeStruct((8, 2, 4, 4...  42.8 us
    pallas_call x1, Pallas kernels, gather_cache(): pl.pallas_call(gather_kernel, out_shape=jax.ShapeDtypeStruct((4, 144, 16...  41.4 us
    dot_general x1, matrix products, on_device(): jnp.dot(query_latent, latent_all, preferred_element_type=jnp.float32)  4.59 us
    ppermute x1, starting transfers between devices, on_device(): w_far = lax.ppermute(w_out, 'ylo', [(0, 1), (1, 0)])  3.61 us
    dot_general x1, matrix products, on_device(): lax.dot_general(weights.astype(jnp.bfloat16), latent_all, (((1,), (1,)),...  2.41 us
  transfers between devices with their start and end apart: 1, of which 0 were waited for; matrix products, arithmetic and copies ran while one was open for 14% of the time, Pallas kernels for 40%

profile of v1, /device:TPU:64, one launch (start us, length us, event | category | flops | bytes accessed | tf_op | source)
XLA Modules:
  0.0 103.4 jit_solution(11857320941843766574)
XLA Ops:
  0.0 0.0 copy-start
  0.0 3.6 %collective-permute-start = (bf16[448,512]{1,0:T(8,128)(2,1)}, bf16[448,512]{1,0:T(8,128)(2,1)S(1)}, u32[]{:S(2)}, u32[]{:S(2)}) collective-permute-start(bf16[448,512]{1,0:T(8,128)(2,1)} %w_near.1), channel_id=1, source_target_pairs={{0,32},{32,0},{1,33},{33,1},{2,34},{34,2},{3,35},{35,3},{4,36},{36... | collective-permute-start | bytes 1376264 | tf_op jit(solution)/shard_map/ppermute | solution.py:376
  3.6 1.0 copy.20
  4.6 0.8 select_reduce_fusion
  5.4 0.7 broadcast_bitcast_fusion
  6.0 41.4 %gather_cache.1 = bf16[4,144,4096]{2,1,0:T(8,128)(2,1)} custom-call(bf16[512,256]{1,0:T(8,128)(2,1)} %lat.1, bf16[64,256]{1,0:T(8,128)(2,1)} %rope.1), custom_call_target="tpu_custom_call" | custom-call | tf_op jit(solution)/shard_map/gather_cache/pallas_call | solution.py:168
  47.4 0.0 copy-done
  47.4 0.0 slice-start
  47.4 1.3 %convolution_convert_fusion = bf16[4,128,512]{2,1,0:T(8,128)(2,1)S(1)} fusion(bf16[4,128,512]{2,1,0:T(8,128)(2,1)S(1)} %copy-done, bf16[128,512]{1,0:T(8,128)(2,1)} %param.9), kind=kOutput, calls=%fused_computation.11 | convolution fusion | flops 67371008 | bytes 1179648 | tf_op jit(solution)/shard_map/rhn,hnl->hrl/dot_general | solution.py:358
  48.8 0.0 slice-start.1
  48.8 4.6 %fusion.8 = f32[512,4096]{1,0:T(8,128)S(1)} fusion(bf16[512,512]{1,0:T(8,128)(2,1)S(1)} %bitcast.41, bf16[576,4096]{1,0:T(8,128)(2,1)} %bitcast.36), kind=kOutput, calls=%fused_computation.9 | convolution fusion | flops 2147483648 | bytes 13107200 | tf_op jit(solution)/shard_map/dot_general | solution.py:378
  53.4 0.0 slice-done
  53.4 0.0 slice-done.1
  53.4 2.1 %fusion.34 = (f32[512]{0:T(512)S(1)}, f32[512,4096]{1,0:T(8,128)S(1)}) fusion(f32[512,4096]{1,0:T(8,128)S(1)} %fusion.8, bf16[4,8,8,128]{3,2,1,0:T(8,128)(2,1)S(1)} %bitcast.44, bf16[576,4096]{1,0:T(8,128)(2,1)S(1)} %bitcast.39, s32[512]{0:T(512)S(1)} %broadcast_bitcast_fusion, s32[4096]{0:T(1024)S(1)} %fusion.32), kind=kOutput, calls=%fused_computation.36 | convolution fusion | flops 278920704 | bytes 17387520 | tf_op jit(solution)/shard_map/dot_general | solution.py:379
  55.5 1.3 %fusion.2 = f32[512]{0:T(512)S(1)} fusion(f32[512,4096]{1,0:T(8,128)S(1)} %get-tuple-element.6, f32[512]{0:T(512)S(1)} %get-tuple-element.5), kind=kLoop, calls=%fused_computation.4 | loop fusion | flops 4193792 | bytes 8392704 | tf_op jit(solution)/shard_map/reduce_sum | solution.py:384
  56.8 0.0 copy-start.2
  56.8 0.0 copy-start.1
  56.8 2.4 %fusion.15 = bf16[512,512]{1,0:T(8,128)(2,1)S(1)} fusion(bf16[576,4096]{1,0:T(8,128)(2,1)S(1)} %bitcast.40, f32[512,4096]{1,0:T(8,128)S(1)} %get-tuple-element.6, f32[512]{0:T(512)S(1)} %get-tuple-element.5, f32[512]{0:T(512)S(1)} %fusion.2), kind=kOutput, calls=%fused_computation.13 | convolution fusion | flops 2152202240 | bytes 13111296 | tf_op jit(solution)/shard_map/dot_general | solution.py:385
  59.2 0.0 copy-done.2
  59.2 0.3 fusion.20
  59.5 0.1 copy.23
  59.6 0.1 reshape.64
  59.8 0.0 collective-permute-done.w_far
  59.8 0.0 copy-done.1
  59.8 42.8 %project.1 = bf16[8,2,4,448]{3,2,1,0:T(4,128)(2,1)S(1)} custom-call(bf16[2,64,512]{2,1,0:T(8,128)(2,1)S(1)} %reshape.65.vals, bf16[448,512]{1,0:T(8,128)(2,1)S(1)} %copy-done.1, bf16[448,512]{1,0:T(8,128)(2,1)S(1)} %collective-permute-done.w_far), custom_call_target="tpu_custom_call" | custom-call | tf_op jit(solution)/shard_map/project/pallas_call | solution.py:321
  102.6 0.1 copy.25
  102.7 0.8 reshape.66
  (5 shorter events, 0.1 us)
Async XLA Ops:
  0.0 47.4 %copy-start = (bf16[4,128,512]{2,1,0:T(8,128)(2,1)S(1)}, bf16[4,128,512]{2,1,0:T(8,128)(2,1)}, u32[]{:S(2)}) copy-start(bf16[4,128,512]{2,1,0:T(8,128)(2,1)} %param.15) | copy-start | bytes 1572868
  0.0 59.8 %collective-permute-start = (bf16[448,512]{1,0:T(8,128)(2,1)}, bf16[448,512]{1,0:T(8,128)(2,1)S(1)}, u32[]{:S(2)}, u32[]{:S(2)}) collective-permute-start(bf16[448,512]{1,0:T(8,128)(2,1)} %w_near.1), channel_id=1, source_target_pairs={{0,32},{32,0},{1,33},{33,1},{2,34},{34,2},{3,35},{35,3},{4,36},{36... | collective-permute-start | bytes 1376264 | tf_op jit(solution)/shard_map/ppermute | solution.py:376
  47.4 6.0 %slice-start = ((s8[4718592]{0:T(1024)(128)(4,1)}), s8[4194304]{0:T(1024)(128)(4,1)S(1)}, s32[]{:S(2)}) async-start(s8[4718592]{0:T(1024)(128)(4,1)} %bitcast.37), calls=%async_computation | async-start | bytes 8388608
  48.8 4.6 %slice-start.1 = ((s8[4718592]{0:T(1024)(128)(4,1)}), s8[524288]{0:T(1024)(128)(4,1)S(1)}, s32[]{:S(2)}) async-start(s8[4718592]{0:T(1024)(128)(4,1)} %bitcast.37), calls=%async_computation.1 | async-start | bytes 1048576
  56.8 2.4 %copy-start.2 = (bf16[4,512,128]{2,1,0:T(8,128)(2,1)S(1)}, bf16[4,512,128]{2,1,0:T(8,128)(2,1)}, u32[]{:S(2)}) copy-start(bf16[4,512,128]{2,1,0:T(8,128)(2,1)} %param.16) | copy-start | bytes 1572868
  56.8 3.0 %copy-start.1 = (bf16[448,512]{1,0:T(8,128)(2,1)S(1)}, bf16[448,512]{1,0:T(8,128)(2,1)}, u32[]{:S(2)}) copy-start(bf16[448,512]{1,0:T(8,128)(2,1)} %w_near.1) | copy-start | bytes 1376260

commit v2 on v0

v2 whole, which is shorter than its diff:
```python
import jax
import jax.numpy as jnp
from jax import lax
from jax.experimental import pallas as pl
from jax.experimental.pallas import tpu as pltpu
from jax.sharding import Mesh
from jax.sharding import PartitionSpec as P

NOPE = 128
ROPE = 64
LATENT = 512
VHEAD = 128
PANEL = 256
KEYS = LATENT + ROPE
AXES = ("z", "ylo", "x", "yhi", "core")
ROW = ("z", "ylo")
HEAD = ("x", "yhi", "core")
MESH = pl.DeviceIdType.MESH
NZ, NX, NY = 8, 4, 4
HEADS, ROWS = 4, 128
SLICE = 448
DZ = (0, 1, 7, 2, 6, 3, 5, 4)
OFF = (0, -1, 1, -2, 2, -3, 3, 4)
SHIFTS = (3, 6, 9, 10)
SUBS = 4
LIMIT = ((4, 4, 3, 3), (3, 3, 4, 4))
ORDER = (
    ("a", 1), ("m", 0), ("a", 2), ("m", 1), ("m", 2), ("c", 0), ("a", 3), ("m", 3), ("m", 4),
    ("c", 1), ("c", 2), ("x", 0), ("a", 4), ("m", 5), ("m", 6), ("c", 3), ("c", 4), ("x", 1),
    ("x", 2), ("m", 7), ("c", 5), ("c", 6), ("x", 3), ("x", 4), ("c", 7), ("x", 5), ("x", 6),
    ("x", 7),
)
LOWEST = -1e30

softmax_scale = 192.0 ** (-0.5)


def mod(a, n):
    return lax.rem(a + n, n)


def remote(src, dst, send_sem, recv_sem, device):
    return pltpu.make_async_remote_copy(
        src_ref=src,
        dst_ref=dst,
        send_sem=send_sem,
        recv_sem=recv_sem,
        device_id=device,
        device_id_type=MESH,
    )


def meet(peers):
    barrier = pltpu.get_barrier_semaphore()
    for peer in peers:
        pl.semaphore_signal(barrier, inc=1, device_id=peer, device_id_type=MESH)
    pl.semaphore_wait(barrier, len(peers))


def kernel(
    q_nope, q_rope, lat, rope, blocks, query_pos, w_uk, w_uv, w_out, out,
    kv, nope, turned, expand, lift, wide, query, best, denom, mixed, vals,
    vall, acc, cs, cr, xs, xr, xown, fs, fr,
    load_sem, send_sem, z_sem, x_sem, y_sem, c_sem, w_sem,
    ag_sem, d_sem, r_sem, f_sem,
):
    z, ylo, x, yhi, c = (lax.axis_index(a) for a in AXES)
    bf, f32 = jnp.bfloat16, jnp.float32
    way = 1 - 2 * c
    here = z * 2 + ylo
    partner = {"core": 1 - c}

    def home(m, d):
        return {"z": mod(z + OFF[m], NZ), "yhi": mod(yhi + d, NY)}

    def piece(panel, half, part):
        return (panel * 2 + half) * 4 + part

    near = pl.ds(pl.multiple_of(SLICE * ylo, SLICE), SLICE)
    loads = []
    for half in range(2):
        lanes = pl.ds(128 * half, 128)
        for part in range(3):
            loads.append((lat.at[pl.ds(144 * part, 144), lanes], kv.at[piece(here, half, part)]))
        last = kv.at[piece(here, half, 3)]
        loads.append((lat.at[pl.ds(432, 80), lanes], last.at[pl.ds(0, 80)]))
        loads.append((rope.at[:, lanes], last.at[pl.ds(80, 64)]))
    loads += [(q_nope, nope), (q_rope, turned), (w_uk, lift), (w_uv, expand), (w_out, wide.at[near])]
    loads = [pltpu.make_async_copy(s, d, load_sem.at[i]) for i, (s, d) in enumerate(loads)]
    for load in loads:
        load.start()
    y_up = {"ylo": 1 - ylo, "yhi": mod(yhi + ylo, NY)}
    y_down = {"ylo": 1 - ylo, "yhi": mod(yhi + ylo - 1, NY)}
    peers = [home(m, d) for m in range(NZ) for d in range(NY) if m or d]
    peers += [{"x": mod(x + d, NX)} for d in range(1, NX)]
    peers += [y_up, y_down, partner]
    meet(peers)
    for load in loads[:10]:
        load.wait()

    def arrived(ref, sem):
        remote(ref, ref, send_sem.at[0], sem, partner).wait_recv()

    mine = kv.at[piece(here, c, x)]
    for d in (1, 7, 2, 6, 3, 5, 4):
        remote(mine, mine, send_sem.at[0], z_sem.at[DZ.index(d)], {"z": mod(z + d, NZ)}).start()

    def panel_of(k, low):
        return mod(z - DZ[k], NZ) * 2 + low

    def spread_y(k, part, turn):
        ref = kv.at[piece(panel_of(k, ylo), c, part)]
        to = {"ylo": 1 - ylo, "yhi": mod(yhi + ylo - lax.rem(part, 2), NY)}
        remote(ref, ref, send_sem.at[0], y_sem.at[k, turn], to).start()

    def spread_core(panel, part, slot):
        ref = kv.at[piece(panel, c, part)]
        remote(ref, ref, send_sem.at[0], c_sem.at[slot], partner).start()

    def spread_x(k, part, turn, step):
        ref = kv.at[piece(panel_of(k, ylo), c, part)]
        remote(ref, ref, send_sem.at[0], x_sem.at[k, turn], {"x": mod(x + step, NX)}).start()

    parts = (x, mod(x - way, NX), mod(x + way, NX), mod(x + 2, NX))

    def stage_z(k):
        if k:
            arrived(kv.at[piece(panel_of(k, ylo), c, x)], z_sem.at[k])
            spread_x(k, x, 0, way)
            spread_x(k, x, 1, -way)
        spread_y(k, x, 0)
        if k:
            spread_core(panel_of(k, ylo), x, k)

    def stage_x(k, turns):
        for turn in turns:
            part = parts[turn + 1]
            if k:
                arrived(kv.at[piece(panel_of(k, ylo), c, part)], x_sem.at[k, turn])
            if k and turn == 0:
                spread_x(k, part, 2, way)
            spread_y(k, part, turn + 1)
            if k:
                spread_core(panel_of(k, ylo), part, k)

    def stage_y(k):
        panel = panel_of(k, 1 - ylo)
        for turn in range(4):
            arrived(kv.at[piece(panel, c, parts[turn])], y_sem.at[k, turn])
            spread_core(panel, parts[turn], 8 + k)

    def stage_core(k):
        if k:
            arrived(kv.at[pl.ds(piece(panel_of(k, ylo), 1 - c, 0), 4)], c_sem.at[k])
        arrived(kv.at[pl.ds(piece(panel_of(k, 1 - ylo), 1 - c, 0), 4)], c_sem.at[8 + k])

    across = lax.broadcasted_iota(jnp.int32, (ROWS, ROWS), 1)
    down = lax.broadcasted_iota(jnp.int32, (ROWS, ROWS), 0)
    row_pos = jnp.sum(
        jnp.where(across == down, query_pos[...].astype(f32), 0.0), axis=1, keepdims=True
    )

    def absorb():
        for load in loads[10:13]:
            load.wait()
        for h in range(HEADS):
            lifted = jnp.dot(
                nope[:, NOPE * h : NOPE * h + NOPE], lift[h], preferred_element_type=f32
            )
            at = slice(ROWS * h, ROWS * h + ROWS)
            query[at, :LATENT] = lifted.astype(bf)
            query[at, LATENT:] = turned[:, ROPE * h : ROPE * h + ROPE]

    def attend(k):
        panels = (panel_of(k, ylo), panel_of(k, 1 - ylo))
        lane = lax.broadcasted_iota(jnp.int32, (1, 128), 1)
        spots = jnp.concatenate(
            [blocks[p] * PANEL + 128 * half + lane for p in panels for half in range(2)], axis=1
        ).astype(f32)

        def one_head(h, carry):
            at = pl.ds(pl.multiple_of(ROWS * h, ROWS), ROWS)
            keys = jnp.concatenate(
                [
                    kv[pl.ds(piece(p, half, 0), 4)].reshape(KEYS, 128)
                    for p in panels
                    for half in range(2)
                ],
                axis=1,
            )
            scores = jnp.dot(query[at, :], keys, preferred_element_type=f32)
            scores = jnp.where(spots <= row_pos, scores * softmax_scale, -jnp.inf)
            top = jnp.max(scores, axis=1, keepdims=True)
            if k:
                before = best[at, :1]
                top = jnp.maximum(before, top)
                shrink = jnp.exp(before - top)
            else:
                top = jnp.maximum(top, LOWEST)
            weights = jnp.exp(scores - top)
            total = jnp.sum(weights, axis=1, keepdims=True)
            update = lax.dot_general(
                weights.astype(bf), keys[:LATENT], (((1,), (1,)), ((), ())),
                preferred_element_type=f32,
            )
            if k:
                total = total + denom[at, :1] * shrink
                update = update + mixed[at, :] * shrink
            best[at, :] = jnp.broadcast_to(top, (ROWS, 128))
            denom[at, :] = jnp.broadcast_to(total, (ROWS, 128))
            mixed[at, :] = update
            return carry

        lax.fori_loop(0, HEADS, one_head, 0)

    for t in range(NZ + SHIFTS[-1]):
        if t < NZ:
            stage_z(t)
        if t == 0:
            absorb()
        if 0 <= t - SHIFTS[0] < NZ:
            stage_x(t - SHIFTS[0], (0, 1))
        if 0 <= t - SHIFTS[1] < NZ:
            stage_x(t - SHIFTS[1], (2,))
        if t == SHIFTS[1] + NZ - 1:
            loads[14].wait()
            remote(
                wide.at[near], wide.at[near], send_sem.at[5], w_sem.at[0], {"ylo": 1 - ylo}
            ).start()
        if 0 <= t - SHIFTS[2] < NZ:
            stage_y(t - SHIFTS[2])
        if 0 <= t - SHIFTS[3] < NZ:
            stage_core(t - SHIFTS[3])
            attend(t - SHIFTS[3])

    loads[13].wait()
    source = ((down % 64) // 4) * 8 + (down // 64) * 4 + down % 4
    order = jnp.where(across == source, 1.0, 0.0).astype(bf)
    for h in range(HEADS):
        at = slice(ROWS * h, ROWS * h + ROWS)
        latent = (mixed[at, :] / denom[at, :1]).astype(bf)
        head = jnp.dot(latent, expand[h], preferred_element_type=f32).astype(bf)
        head = jnp.dot(order, head, preferred_element_type=f32).astype(bf)
        vals[:, :, VHEAD * h : VHEAD * h + VHEAD] = head.reshape(SUBS, ROWS // SUBS, VHEAD)

    steps = ({"z": mod(z + 1, NZ)}, {"z": mod(z - 1, NZ)})

    for sub in range(SUBS):
        for side in range(2):
            remote(
                vals.at[sub], vall.at[SUBS * z + sub], send_sem.at[1], ag_sem.at[side, 0, sub],
                steps[side],
            ).start()

    def land(dist):
        for sub in range(SUBS):
            for side in range(2):
                if dist > LIMIT[side][sub]:
                    continue
                source = mod(z + (dist if side else -dist), NZ)
                ref = vall.at[SUBS * source + sub]
                arrived(ref, ag_sem.at[side, dist - 1, sub])
                if dist + 1 <= LIMIT[side][sub]:
                    remote(
                        ref, ref, send_sem.at[1], ag_sem.at[side, dist, sub], steps[side]
                    ).start()

    def multiply(m):
        if m:
            rows = vall[pl.ds(SUBS * mod(z + OFF[m], NZ), SUBS)].reshape(128, 512)
        else:
            rows = vals[...].reshape(128, 512)
        product = lax.dot_general(
            rows, wide[...], (((1,), (1,)), ((), ())), preferred_element_type=f32
        )
        acc[m] = product.reshape(2, 64, 2 * SLICE)
        cs[m] = acc[m, 1 - c].astype(bf)
        remote(cs.at[m], cr.at[m], send_sem.at[2], d_sem.at[m], partner).start()

    def reduce_core(m):
        arrived(cr.at[m], d_sem.at[m])
        for d in (2, 1, 3, 0):
            at = pl.ds(pl.multiple_of(16 * mod(x + d, NX), 16), 16)
            both = acc[m, c, at, :] + cr[m, at, :].astype(f32)
            if d:
                xs[m, d - 1] = both.astype(bf)
            else:
                xown[m] = both
            if d:
                remote(
                    xs.at[m, d - 1], xr.at[m, d - 1], send_sem.at[3], r_sem.at[m, d - 1],
                    {"x": mod(x + d, NX)},
                ).start()

    def reduce_x(m):
        for d in range(3):
            arrived(xr.at[m, d], r_sem.at[m, d])
        total = xown[m]
        for d in range(3):
            total = total + xr[m, d].astype(f32)
        for y in range(NY):
            fs[NY * m + y] = total[4 * y : 4 * y + 4].astype(bf)
        for d in (2, 1, 3, 0):
            ref = fs.at[NY * m + mod(yhi + d, NY)]
            if m or d:
                remote(ref, fr.at[m, d], send_sem.at[4], f_sem.at[m, d], home(m, d)).start()
            else:
                fr[0, 0] = fs[yhi]

    far = pl.ds(pl.multiple_of(SLICE * (1 - ylo), SLICE), SLICE)
    for step in ORDER:
        if step == ("m", 0):
            arrived(wide.at[far], w_sem.at[0])
        {"a": land, "m": multiply, "c": reduce_core, "x": reduce_x}[step[0]](step[1])
    for m in range(NZ):
        for d in range(NY):
            if m or d:
                arrived(fr.at[m, d], f_sem.at[m, d])
        total = fr[m, 0].astype(f32)
        for d in range(1, NY):
            total = total + fr[m, d].astype(f32)
        out[mod(z - OFF[m], NZ)] = total.astype(bf)
    pieces = kv.at[pl.ds(0, 7 + 21 + 32 + 28 + 32)]
    sent = (pieces, vall.at[pl.ds(0, 7 * SUBS)], cs, xs, fs.at[pl.ds(0, 31)], wide.at[near])
    for i, ref in enumerate(sent):
        remote(ref, ref, send_sem.at[i], w_sem.at[0], partner).wait_send()


def attention(*operands):
    bf, f32 = jnp.bfloat16, jnp.float32
    anywhere = pl.BlockSpec(memory_space=pl.ANY)
    vmem = pl.BlockSpec(memory_space=pltpu.VMEM)
    smem = pl.BlockSpec(memory_space=pltpu.SMEM)
    return pl.pallas_call(
        kernel,
        out_shape=jax.ShapeDtypeStruct((8, 4, 2 * SLICE), bf),
        in_specs=[anywhere] * 4 + [smem, vmem] + [anywhere] * 3,
        out_specs=vmem,
        scratch_shapes=[
            pltpu.VMEM((128, 144, 128), bf),
            pltpu.VMEM((ROWS, HEADS * NOPE), bf),
            pltpu.VMEM((ROWS, HEADS * ROPE), bf),
            pltpu.VMEM((HEADS, LATENT, VHEAD), bf),
            pltpu.VMEM((HEADS, NOPE, LATENT), bf),
            pltpu.VMEM((2 * SLICE, HEADS * VHEAD), bf),
            pltpu.VMEM((HEADS * ROWS, KEYS), bf),
            pltpu.VMEM((HEADS * ROWS, 128), f32),
            pltpu.VMEM((HEADS * ROWS, 128), f32),
            pltpu.VMEM((HEADS * ROWS, LATENT), f32),
            pltpu.VMEM((SUBS, ROWS // SUBS, HEADS * VHEAD), bf),
            pltpu.VMEM((NZ * SUBS, ROWS // SUBS, HEADS * VHEAD), bf),
            pltpu.VMEM((8, 2, 64, 2 * SLICE), f32),
            pltpu.VMEM((8, 64, 2 * SLICE), bf),
            pltpu.VMEM((8, 64, 2 * SLICE), bf),
            pltpu.VMEM((8, 3, 16, 2 * SLICE), bf),
            pltpu.VMEM((8, 3, 16, 2 * SLICE), bf),
            pltpu.VMEM((8, 16, 2 * SLICE), f32),
            pltpu.VMEM((32, 4, 2 * SLICE), bf),
            pltpu.VMEM((8, 4, 4, 2 * SLICE), bf),
            pltpu.SemaphoreType.DMA((15,)),
            pltpu.SemaphoreType.DMA((6,)),
            pltpu.SemaphoreType.DMA((8,)),
            pltpu.SemaphoreType.DMA((8, 3)),
            pltpu.SemaphoreType.DMA((8, 4)),
            pltpu.SemaphoreType.DMA((16,)),
            pltpu.SemaphoreType.DMA((1,)),
            pltpu.SemaphoreType.DMA((2, 4, SUBS)),
            pltpu.SemaphoreType.DMA((8,)),
            pltpu.SemaphoreType.DMA((8, 3)),
            pltpu.SemaphoreType.DMA((8, 4)),
        ],
        compiler_params=pltpu.CompilerParams(
            collective_id=0, has_side_effects=True, vmem_limit_bytes=56 << 20
        ),
        name="attention",
    )(*operands)


def on_device(q_nope, q_rope, latent_keys, rope_keys, panel_block, query_pos, w_uk, w_uv, w_out):
    pieces = attention(
        q_nope, q_rope, latent_keys, rope_keys, panel_block, query_pos.reshape(1, ROWS),
        w_uk, w_uv, w_out,
    )
    return jnp.transpose(pieces, (1, 0, 2)).reshape(4, NZ * 2 * SLICE)


def solution(mesh):
    finer = Mesh(mesh.devices.reshape(NZ, 2, NX, NY, 2), AXES)
    return jax.shard_map(
        on_device,
        mesh=finer,
        in_specs=(
            P(ROW, HEAD),
            P(ROW, HEAD),
            P(None, ROW),
            P(None, ROW),
            P(),
            P(ROW),
            P(HEAD, None, None),
            P(HEAD, None, None),
            P(ROW, HEAD),
        ),
        out_specs=P(ROW + HEAD, None),
        check_vma=False,
    )
```

time: 270 us -> 89.9 us (0.33)
  waiting for transfers between devices: 115 us -> 0 us
  blocking collectives: 112 us -> 0 us
  Pallas kernels: 0 us -> 88.2 us
  matrix products: 14.7 us -> 0 us
  between operations: 13.5 us -> 0.01 us
  local copies, waits for them, and re-layouts: 9.19 us -> 1.46 us
  other arithmetic: 6.12 us -> 0 us
    all_gather x1 -> x0, waiting for transfers between devices: 114 us -> none  [in_one_piece(): lax.all_gather(both, axis, axis=dim, tiled=True)]
    all_to_all x4 -> x0, blocking collectives: 112 us -> none  [the longest x1 56.4 us: from_everyone(): lax.all_to_all(jnp.broadcast_to(x[None], (count, *x.shape)), axis, 0, 0,...]
    pallas_call x0 -> x1, Pallas kernels: none -> 88.2 us  [attention(): pl.pallas_call(kernel, out_shape=jax.ShapeDtypeStruct((8, 4, 2 * SLICE),...]
    dot_general x6 -> x0, matrix products: 14.7 us -> none  [the longest x1 4.68 us: on_device(): jnp.dot(query_latent, latent_piece, preferred_element_type=jnp.float32)]
    reduce_sum x4 -> x0, other arithmetic: 4.35 us -> none  [the longest x1 1.78 us: summed_on_arrival(): return arrived.astype(jnp.float32).sum(axis=0)]
    reshape x3 -> x0, local copies, waits for them, and re-layouts: 4.03 us -> none  [the longest x2 3.27 us: split_up(): return jnp.moveaxis(x.reshape(*before, count, -1, *after), dim, 0)]
  transfers between devices with their start and end apart: 1 -> 0, of which waited for: 1 -> 0; matrix products, arithmetic and copies ran while one was open for 1% -> 0% of each run, Pallas kernels for 0% -> 0%
where the time goes in v2:
time: 89.9 us; the launch traced here: 89.7 us
  Pallas kernels  88.2 us (98%)
  local copies, waits for them, and re-layouts  1.46 us (2%)
    pallas_call x1, Pallas kernels, attention(): pl.pallas_call(kernel, out_shape=jax.ShapeDtypeStruct((8, 4, 2 * SLICE),...  88.2 us

profile of v2, /device:TPU:8, one launch (start us, length us, event | category | flops | bytes accessed | tf_op | source)
XLA Modules:
  0.0 89.7 jit_solution(6301723399755902462)
XLA Ops:
  0.0 88.2 %attention.1 = bf16[8,4,896]{2,1,0:T(4,128)(2,1)} custom-call(bf16[128,512]{1,0:T(8,128)(2,1)} %q_nope.1, bf16[128,256]{1,0:T(8,128)(2,1)} %q_rope.1, bf16[512,256]{1,0:T(8,128)(2,1)} %lat.1, bf16[64,256]{1,0:T(8,128)(2,1)} %rope.1, s32[16]{0:T(128)} %blocks.1, s32[1,128]{1,0:T(1,128)} %bitcast.5, bf16[4,128,512]{2,1,0:T(8,128)(2,1)} %w_uk.1, ...), custom_call_target="tpu_custom_call" | custom-call | tf_op jit(solution)/shard_map/attention/pallas_call | solution.py:334
  88.2 1.5 %copy.11 = bf16[4,7168]{1,0:T(4,128)(2,1)} copy(bf16[4,7168]{1,0:T(4,128)(2,1)} %bitcast.4) | data formatting | bytes 114688

commit v3 on v2

--- a/solution.py
+++ b/solution.py
@@ -21,7 +21,9 @@
 SLICE = 448
 DZ = (0, 1, 7, 2, 6, 3, 5, 4)
 OFF = (0, -1, 1, -2, 2, -3, 3, 4)
-SHIFTS = (3, 6, 9, 10)
+SHIFTS = (3, 5, 7, 8)
+SHARES = (8, 9, 10, 11)
+BLOCK = 256
 SUBS = 4
 LIMIT = ((4, 4, 3, 3), (3, 3, 4, 4))
 ORDER = (
@@ -154,11 +156,17 @@
             arrived(kv.at[pl.ds(piece(panel_of(k, ylo), 1 - c, 0), 4)], c_sem.at[k])
         arrived(kv.at[pl.ds(piece(panel_of(k, 1 - ylo), 1 - c, 0), 4)], c_sem.at[8 + k])
 
+    def share(quarter):
+        ref = wide.at[pl.ds(pl.multiple_of(SLICE * ylo + 112 * quarter, 16), 112)]
+        remote(ref, ref, send_sem.at[5], w_sem.at[quarter], {"ylo": 1 - ylo}).start()
+
     across = lax.broadcasted_iota(jnp.int32, (ROWS, ROWS), 1)
     down = lax.broadcasted_iota(jnp.int32, (ROWS, ROWS), 0)
     row_pos = jnp.sum(
         jnp.where(across == down, query_pos[...].astype(f32), 0.0), axis=1, keepdims=True
     )
+
+    rows_pos = jnp.concatenate([row_pos] * (BLOCK // ROWS), axis=0)
 
     def absorb():
         for load in loads[10:13]:
@@ -178,8 +186,8 @@
             [blocks[p] * PANEL + 128 * half + lane for p in panels for half in range(2)], axis=1
         ).astype(f32)
 
-        def one_head(h, carry):
-            at = pl.ds(pl.multiple_of(ROWS * h, ROWS), ROWS)
+        def one_block(b, carry):
+            at = pl.ds(pl.multiple_of(BLOCK * b, BLOCK), BLOCK)
             keys = jnp.concatenate(
                 [
                     kv[pl.ds(piece(p, half, 0), 4)].reshape(KEYS, 128)
@@ -189,7 +197,7 @@
                 axis=1,
             )
             scores = jnp.dot(query[at, :], keys, preferred_element_type=f32)
-            scores = jnp.where(spots <= row_pos, scores * softmax_scale, -jnp.inf)
+            scores = jnp.where(spots <= rows_pos, scores * softmax_scale, -jnp.inf)
             top = jnp.max(scores, axis=1, keepdims=True)
             if k:
                 before = best[at, :1]
@@ -206,27 +214,25 @@
             if k:
                 total = total + denom[at, :1] * shrink
                 update = update + mixed[at, :] * shrink
-            best[at, :] = jnp.broadcast_to(top, (ROWS, 128))
-            denom[at, :] = jnp.broadcast_to(total, (ROWS, 128))
+            best[at, :] = jnp.broadcast_to(top, (BLOCK, 128))
+            denom[at, :] = jnp.broadcast_to(total, (BLOCK, 128))
             mixed[at, :] = update
             return carry
 
-        lax.fori_loop(0, HEADS, one_head, 0)
+        lax.fori_loop(0, HEADS * ROWS // BLOCK, one_block, 0)
 
     for t in range(NZ + SHIFTS[-1]):
         if t < NZ:
             stage_z(t)
         if t == 0:
             absorb()
+            loads[14].wait()
         if 0 <= t - SHIFTS[0] < NZ:
             stage_x(t - SHIFTS[0], (0, 1))
         if 0 <= t - SHIFTS[1] < NZ:
             stage_x(t - SHIFTS[1], (2,))
-        if t == SHIFTS[1] + NZ - 1:
-            loads[14].wait()
-            remote(
-                wide.at[near], wide.at[near], send_sem.at[5], w_sem.at[0], {"ylo": 1 - ylo}
-            ).start()
+        if t in SHARES:
+            share(SHARES.index(t))
         if 0 <= t - SHIFTS[2] < NZ:
             stage_y(t - SHIFTS[2])
         if 0 <= t - SHIFTS[3] < NZ:
@@ -307,10 +313,11 @@
             else:
                 fr[0, 0] = fs[yhi]
 
-    far = pl.ds(pl.multiple_of(SLICE * (1 - ylo), SLICE), SLICE)
     for step in ORDER:
         if step == ("m", 0):
-            arrived(wide.at[far], w_sem.at[0])
+            for quarter in range(4):
+                away = pl.multiple_of(SLICE * (1 - ylo) + 112 * quarter, 16)
+                arrived(wide.at[pl.ds(away, 112)], w_sem.at[quarter])
         {"a": land, "m": multiply, "c": reduce_core, "x": reduce_x}[step[0]](step[1])
     for m in range(NZ):
         for d in range(NY):
@@ -319,7 +326,8 @@
         total = fr[m, 0].astype(f32)
         for d in range(1, NY):
             total = total + fr[m, d].astype(f32)
-        out[mod(z - OFF[m], NZ)] = total.astype(bf)
+        at = pl.multiple_of(2 * SLICE * mod(z - OFF[m], NZ), 2 * SLICE)
+        out[:, pl.ds(at, 2 * SLICE)] = total.astype(bf)
     pieces = kv.at[pl.ds(0, 7 + 21 + 32 + 28 + 32)]
     sent = (pieces, vall.at[pl.ds(0, 7 * SUBS)], cs, xs, fs.at[pl.ds(0, 31)], wide.at[near])
     for i, ref in enumerate(sent):
@@ -333,7 +341,7 @@
     smem = pl.BlockSpec(memory_space=pltpu.SMEM)
     return pl.pallas_call(
         kernel,
-        out_shape=jax.ShapeDtypeStruct((8, 4, 2 * SLICE), bf),
+        out_shape=jax.ShapeDtypeStruct((4, NZ * 2 * SLICE), bf),
         in_specs=[anywhere] * 4 + [smem, vmem] + [anywhere] * 3,
         out_specs=vmem,
         scratch_shapes=[
@@ -363,7 +371,7 @@
             pltpu.SemaphoreType.DMA((8, 3)),
             pltpu.SemaphoreType.DMA((8, 4)),
             pltpu.SemaphoreType.DMA((16,)),
-            pltpu.SemaphoreType.DMA((1,)),
+            pltpu.SemaphoreType.DMA((4,)),
             pltpu.SemaphoreType.DMA((2, 4, SUBS)),
             pltpu.SemaphoreType.DMA((8,)),
             pltpu.SemaphoreType.DMA((8, 3)),
@@ -377,11 +385,10 @@
 
 
 def on_device(q_nope, q_rope, latent_keys, rope_keys, panel_block, query_pos, w_uk, w_uv, w_out):
-    pieces = attention(
+    return attention(
         q_nope, q_rope, latent_keys, rope_keys, panel_block, query_pos.reshape(1, ROWS),
         w_uk, w_uv, w_out,
     )
-    return jnp.transpose(pieces, (1, 0, 2)).reshape(4, NZ * 2 * SLICE)
 
 
 def solution(mesh):

time: 89.9 us -> 85.5 us (0.951)
  the two profiles are of different devices: /device:TPU:8 before, /device:TPU:16 now
where the time goes in v3:
time: 85.5 us; the launch traced here: 85.4 us
  Pallas kernels  83.9 us (98%)
  local copies, waits for them, and re-layouts  1.46 us (2%)
    pallas_call x1, Pallas kernels, attention(): pl.pallas_call(kernel, out_shape=jax.ShapeDtypeStruct((4, NZ * 2 * SLICE)...  83.9 us

profile of v3, /device:TPU:16, one launch (start us, length us, event | category | flops | bytes accessed | tf_op | source)
XLA Modules:
  0.0 85.4 jit_solution(5036222761743576423)
XLA Ops:
  0.0 83.9 %attention.1 = bf16[4,7168]{1,0:T(4,128)(2,1)} custom-call(bf16[128,512]{1,0:T(8,128)(2,1)} %q_nope.1, bf16[128,256]{1,0:T(8,128)(2,1)} %q_rope.1, bf16[512,256]{1,0:T(8,128)(2,1)} %lat.1, bf16[64,256]{1,0:T(8,128)(2,1)} %rope.1, s32[16]{0:T(128)} %blocks.1, s32[1,128]{1,0:T(1,128)} %bitcast.1, bf16[4,128,512]{2,1,0:T(8,128)(2,1)} %w_uk.1, ...), custom_call_target="tpu_custom_call" | custom-call | tf_op jit(solution)/shard_map/attention/pallas_call | solution.py:342
  83.9 1.5 %copy.11 = bf16[4,7168]{1,0:T(4,128)(2,1)} copy(bf16[4,7168]{1,0:T(4,128)(2,1)} %attention.1) | data formatting | bytes 114688

commit v4 on v3

--- a/solution.py
+++ b/solution.py
@@ -22,7 +22,7 @@
 DZ = (0, 1, 7, 2, 6, 3, 5, 4)
 OFF = (0, -1, 1, -2, 2, -3, 3, 4)
 SHIFTS = (3, 5, 7, 8)
-SHARES = (8, 9, 10, 11)
+SHARES = (10, 11, 12, 13)
 BLOCK = 256
 SUBS = 4
 LIMIT = ((4, 4, 3, 3), (3, 3, 4, 4))
@@ -224,7 +224,7 @@
     for t in range(NZ + SHIFTS[-1]):
         if t < NZ:
             stage_z(t)
-        if t == 0:
+        if t == 2:
             absorb()
             loads[14].wait()
         if 0 <= t - SHIFTS[0] < NZ:
@@ -239,27 +239,28 @@
             stage_core(t - SHIFTS[3])
             attend(t - SHIFTS[3])
 
-    loads[13].wait()
-    source = ((down % 64) // 4) * 8 + (down // 64) * 4 + down % 4
-    order = jnp.where(across == source, 1.0, 0.0).astype(bf)
-    for h in range(HEADS):
-        at = slice(ROWS * h, ROWS * h + ROWS)
-        latent = (mixed[at, :] / denom[at, :1]).astype(bf)
-        head = jnp.dot(latent, expand[h], preferred_element_type=f32).astype(bf)
-        head = jnp.dot(order, head, preferred_element_type=f32).astype(bf)
-        vals[:, :, VHEAD * h : VHEAD * h + VHEAD] = head.reshape(SUBS, ROWS // SUBS, VHEAD)
-
     steps = ({"z": mod(z + 1, NZ)}, {"z": mod(z - 1, NZ)})
 
-    for sub in range(SUBS):
+    def publish(sub):
         for side in range(2):
             remote(
                 vals.at[sub], vall.at[SUBS * z + sub], send_sem.at[1], ag_sem.at[side, 0, sub],
                 steps[side],
             ).start()
 
+    loads[13].wait()
+    source = ((down % 64) // 4) * 8 + (down // 64) * 4 + down % 4
+    order = jnp.where(across == source, 1.0, 0.0).astype(bf)
+    for h in (0, 2, 1, 3):
+        at = slice(ROWS * h, ROWS * h + ROWS)
+        latent = (mixed[at, :] / denom[at, :1]).astype(bf)
+        head = jnp.dot(latent, expand[h], preferred_element_type=f32).astype(bf)
+        head = jnp.dot(order, head, preferred_element_type=f32).astype(bf)
+        vals[h] = head
+        publish(h)
+
     def land(dist):
-        for sub in range(SUBS):
+        for sub in (0, 2, 1, 3):
             for side in range(2):
                 if dist > LIMIT[side][sub]:
                     continue
@@ -272,10 +273,8 @@
                     ).start()
 
     def multiply(m):
-        if m:
-            rows = vall[pl.ds(SUBS * mod(z + OFF[m], NZ), SUBS)].reshape(128, 512)
-        else:
-            rows = vals[...].reshape(128, 512)
+        held = [vall.at[SUBS * mod(z + OFF[m], NZ) + h] if m else vals.at[h] for h in range(HEADS)]
+        rows = jnp.concatenate([ref[...] for ref in held], axis=1)
         product = lax.dot_general(
             rows, wide[...], (((1,), (1,)), ((), ())), preferred_element_type=f32
         )
@@ -355,8 +354,8 @@
             pltpu.VMEM((HEADS * ROWS, 128), f32),
             pltpu.VMEM((HEADS * ROWS, 128), f32),
             pltpu.VMEM((HEADS * ROWS, LATENT), f32),
-            pltpu.VMEM((SUBS, ROWS // SUBS, HEADS * VHEAD), bf),
-            pltpu.VMEM((NZ * SUBS, ROWS // SUBS, HEADS * VHEAD), bf),
+            pltpu.VMEM((SUBS, ROWS, VHEAD), bf),
+            pltpu.VMEM((NZ * SUBS, ROWS, VHEAD), bf),
             pltpu.VMEM((8, 2, 64, 2 * SLICE), f32),
             pltpu.VMEM((8, 64, 2 * SLICE), bf),
             pltpu.VMEM((8, 64, 2 * SLICE), bf),

time: 85.5 us -> 84.9 us (level)
  no operation moved by 1% of the time
where the time goes in v4:
time: 84.9 us; the launch traced here: 84.7 us
  Pallas kernels  83.3 us (98%)
  local copies, waits for them, and re-layouts  1.46 us (2%)
    pallas_call x1, Pallas kernels, attention(): pl.pallas_call(kernel, out_shape=jax.ShapeDtypeStruct((4, NZ * 2 * SLICE)...  83.3 us

profile of v4, /device:TPU:16, one launch (start us, length us, event | category | flops | bytes accessed | tf_op | source)
XLA Modules:
  0.0 84.7 jit_solution(11732528724504148821)
XLA Ops:
  0.0 83.3 %attention.1 = bf16[4,7168]{1,0:T(4,128)(2,1)} custom-call(bf16[128,512]{1,0:T(8,128)(2,1)} %q_nope.1, bf16[128,256]{1,0:T(8,128)(2,1)} %q_rope.1, bf16[512,256]{1,0:T(8,128)(2,1)} %lat.1, bf16[64,256]{1,0:T(8,128)(2,1)} %rope.1, s32[16]{0:T(128)} %blocks.1, s32[1,128]{1,0:T(1,128)} %bitcast.1, bf16[4,128,512]{2,1,0:T(8,128)(2,1)} %w_uk.1, ...), custom_call_target="tpu_custom_call" | custom-call | tf_op jit(solution)/shard_map/attention/pallas_call | solution.py:341
  83.3 1.5 %copy.11 = bf16[4,7168]{1,0:T(4,128)(2,1)} copy(bf16[4,7168]{1,0:T(4,128)(2,1)} %attention.1) | data formatting | bytes 114688

commit v5 on v4

--- a/solution.py
+++ b/solution.py
@@ -253,7 +253,7 @@
     order = jnp.where(across == source, 1.0, 0.0).astype(bf)
     for h in (0, 2, 1, 3):
         at = slice(ROWS * h, ROWS * h + ROWS)
-        latent = (mixed[at, :] / denom[at, :1]).astype(bf)
+        latent = (mixed[at, :] * (1.0 / denom[at, :1])).astype(bf)
         head = jnp.dot(latent, expand[h], preferred_element_type=f32).astype(bf)
         head = jnp.dot(order, head, preferred_element_type=f32).astype(bf)
         vals[h] = head

time: 84.9 us -> 84.9 us (level)
  no operation moved by 1% of the time
where the time goes in v5:
time: 84.9 us; the launch traced here: 84.7 us
  Pallas kernels  83.3 us (98%)
  local copies, waits for them, and re-layouts  1.46 us (2%)
    pallas_call x1, Pallas kernels, attention(): pl.pallas_call(kernel, out_shape=jax.ShapeDtypeStruct((4, NZ * 2 * SLICE)...  83.3 us

profile of v5, /device:TPU:16, one launch (start us, length us, event | category | flops | bytes accessed | tf_op | source)
XLA Modules:
  0.0 84.7 jit_solution(12870894477818391924)
XLA Ops:
  0.0 83.3 %attention.1 = bf16[4,7168]{1,0:T(4,128)(2,1)} custom-call(bf16[128,512]{1,0:T(8,128)(2,1)} %q_nope.1, bf16[128,256]{1,0:T(8,128)(2,1)} %q_rope.1, bf16[512,256]{1,0:T(8,128)(2,1)} %lat.1, bf16[64,256]{1,0:T(8,128)(2,1)} %rope.1, s32[16]{0:T(128)} %blocks.1, s32[1,128]{1,0:T(1,128)} %bitcast.1, bf16[4,128,512]{2,1,0:T(8,128)(2,1)} %w_uk.1, ...), custom_call_target="tpu_custom_call" | custom-call | tf_op jit(solution)/shard_map/attention/pallas_call | solution.py:341
  83.3 1.5 %copy.11 = bf16[4,7168]{1,0:T(4,128)(2,1)} copy(bf16[4,7168]{1,0:T(4,128)(2,1)} %attention.1) | data formatting | bytes 114688
